TPU v7x, 32 devices: a whole 2x2x4 slice. The times are simulated.
32 devices in a mesh: gz: 4 (over z), gx: 4 (over y, x), gy: 2 (over core).
Axes of the slice: x: 2, y: 2, z: 4, core: 2. Of those that a mesh axis runs over, the one named last changes fastest.
Arguments:
- density: float32 [128, 256, 1024], P('gz', 'gy', 'gx'), may hold values from 0 to 1
- mask: int32 [16, 32, 128], P('gz', 'gy', 'gx'), may hold values from 0 to 3
Outputs:
- filtered: float32 [128, 256, 1024], P(('gz', 'gx'), 'gy')
- projected: float32 [128, 256, 1024], P(('gz', 'gx'), 'gy')
Inputs may be any that keep to these rules, and one draw needn't show every extreme that they name: `mask`: code 0 marks a void block, 1 a solid block, 2 and 3 design blocks.
All inputs are finite; a program needn't handle non-finite values.
Results may differ from a plain program's by a relative error of at most 0.0003.
Values sent between devices are 32-bit elements; how exact they have to be, the bound alone decides.
A program may use at most 128 MiB of HBM per device.

v0:
```python
import jax
import jax.numpy as jnp
from jax import lax
from jax.sharding import PartitionSpec as P

RADIUS = 6
CELLS = 8
sharpness = 8.0
threshold = 0.5
highest = lax.Precision.HIGHEST


def with_halo(x, sides, width):
    for axis, dim in sides:
        peers, length = (lax.axis_size(axis), x.shape[dim])
        up = [(i, (i + 1) % peers) for i in range(peers - 1)]
        down = [(j, i) for i, j in up]
        last = lax.slice_in_dim(x, length - width, length, axis=dim)
        leading = lax.slice_in_dim(x, 0, width, axis=dim)
        before = lax.ppermute(last, axis, up)
        after = lax.ppermute(leading, axis, down)
        x = jnp.concatenate([before, x, after], axis=dim)
    return x


def passed_along(block, axis, distance):
    devices = range(lax.axis_size(axis))
    route = [(i - distance, i) for i in devices if i - distance in devices]
    return lax.ppermute(block, axis, route)


def band(outputs, inputs, shift):
    out_index = lax.broadcasted_iota(jnp.int32, (outputs, inputs), 0)
    in_index = lax.broadcasted_iota(jnp.int32, (outputs, inputs), 1)
    distance = jnp.abs(in_index + shift - out_index)
    return jnp.where(distance <= RADIUS, (RADIUS + 1 - distance).astype(jnp.float32), 0.0)


def along_first(extended, count):
    kernel = band(count, count + 2 * RADIUS, -RADIUS)
    flat = extended.reshape(count + 2 * RADIUS, -1)
    result = jnp.dot(kernel, flat, precision=highest, preferred_element_type=jnp.float32)
    return result.reshape((count,) + extended.shape[1:])


def filter_last(values):
    leading = values.shape[:-1]
    extent = values.shape[-1]
    blocks = extent // 128
    widths = [(0, 0)] * (values.ndim - 1) + [(RADIUS, 128 - RADIUS)]
    padded = jnp.pad(values, widths)
    lower_part = padded[..., :extent].reshape(leading + (blocks, 128))
    upper_part = padded[..., 128 : extent + 128].reshape(leading + (blocks, 128))[..., : 2 * RADIUS]
    lower_kernel = band(128, 128, -RADIUS).T
    upper_kernel = band(128, 2 * RADIUS, 128 - RADIUS).T
    result = jnp.einsum(
        "abcd,de->abce",
        lower_part,
        lower_kernel,
        precision=highest,
        preferred_element_type=jnp.float32,
    )
    result = result + jnp.einsum(
        "abcd,de->abce",
        upper_part,
        upper_kernel,
        precision=highest,
        preferred_element_type=jnp.float32,
    )
    return result.reshape(leading + (extent,))


def one_side(reach):
    return reach * (RADIUS + 1) - reach * (reach + 1) // 2


def edge_sums(start, length, length_all):
    position = start + lax.iota(jnp.int32, length)
    reach_left = jnp.minimum(position, RADIUS)
    reach_right = jnp.minimum(length_all - 1 - position, RADIUS)
    return (RADIUS + 1 + one_side(reach_left) + one_side(reach_right)).astype(jnp.float32)


def body(density, mask):
    planes, row_count, columns = density.shape
    design_code = jnp.repeat(jnp.repeat(jnp.repeat(mask, CELLS, 0), CELLS, 1), CELLS, 2)
    physical = jnp.where(design_code == 0, 0.0, jnp.where(design_code == 1, 1.0, density))
    extended = with_halo(physical, (("gz", 0),), RADIUS)
    physical = along_first(extended, planes)
    groups = lax.axis_size("gx")
    layers = planes // groups
    gathered = lax.all_gather(physical, "gx", axis=2, tiled=True)
    own_slab = lax.dynamic_slice_in_dim(gathered, lax.axis_index("gx") * layers, layers, 0)
    smoothed = filter_last(own_slab)
    row_kernel = band(row_count + 2 * RADIUS, row_count, RADIUS)
    partial_value = jnp.einsum(
        "wy,zyx->zwx", row_kernel, smoothed, precision=highest, preferred_element_type=jnp.float32
    )
    from_previous = passed_along(partial_value[:, row_count + RADIUS :], "gy", 1)
    from_next = passed_along(partial_value[:, :RADIUS], "gy", -1)
    summed = partial_value[:, RADIUS : row_count + RADIUS]
    summed = summed.at[:, :RADIUS].add(from_previous)
    summed = summed.at[:, row_count - RADIUS :].add(from_next)
    width_all = summed.shape[2]
    count_x = edge_sums(0, width_all, width_all)
    count_y = edge_sums(
        lax.axis_index("gy") * row_count, row_count, row_count * lax.axis_size("gy")
    )
    count_z = edge_sums(lax.axis_index(("gz", "gx")) * layers, layers, planes * lax.axis_size("gz"))
    counts = count_z[:, None, None] * count_y[None, :, None] * count_x[None, None, :]
    filtered = summed / counts
    top = jnp.tanh(sharpness * threshold)
    projected = (top + jnp.tanh(sharpness * (filtered - threshold))) / (
        top + jnp.tanh(sharpness * (1.0 - threshold))
    )
    return (filtered, projected)


def solution(mesh):
    placed = (P("gz", "gy", "gx"), P("gz", "gy", "gx"))
    return jax.shard_map(
        body,
        mesh=mesh,
        in_specs=placed,
        out_specs=(P(("gz", "gx"), "gy", None), P(("gz", "gx"), "gy", None)),
        check_vma=False,
    )
```

profile of v0, /device:TPU:1, one launch (start us, length us, event | category | flops | bytes accessed | tf_op | source)
XLA Modules:
  0.0 268.6 jit_solution(17952805797014648781)
XLA Ops:
  7.2 0.0 copy-start
  7.2 0.0 all-gather.2.cloned.1.call-start
  7.2 5.6 %copy.16 = f32[32,128,256]{1,2,0:T(8,128)} copy(f32[32,128,256]{2,1,0:T(8,128)} %param.6) | data formatting | bytes 8388608 | tf_op args[0]
  12.8 0.0 copy-done
  12.8 0.3 broadcast_bitcast_fusion
  13.1 0.6 copy.15
  13.8 0.3 broadcast_bitcast_fusion.1
  14.1 0.6 copy.14
  14.8 3.3 %select_select_fusion = f32[32,128,256]{1,2,0:T(8,128)S(1)} fusion(f32[32,128,256]{1,2,0:T(8,128)} %copy.16, pred[32,128,32]{1,2,0:T(8,128)(4,1)S(1)} %copy.15, pred[32,128,32]{1,2,0:T(8,128)(4,1)S(1)} %copy.14), kind=kLoop, calls=%fused_computation.14 | loop fusion | flops 2097152 | bytes 8650752 | tf_op jit(solution)/shard_map/jit(_where)/select_n | solution.py:87
  18.0 0.1 fusion.86
  18.2 1.3 collective-permute-start.1
  19.5 4.7 %collective-permute-start = (f32[6,128,256]{1,2,0:T(8,128)S(1)}, f32[6,128,256]{1,2,0:T(8,128)S(1)}, u32[]{:S(2)}, u32[]{:S(2)}) collective-permute-start(f32[6,128,256]{1,2,0:T(8,128)S(1)} %get-tuple-element.32), channel_id=1, source_target_pairs={{0,8},{8,16},{16,24},{1,9},{9,17},{17,25},{2,10},{10,18},{18,26},{... | collective-permute-start | bytes 2359304 | tf_op jit(solution)/shard_map/ppermute | solution.py:20
  24.2 15.2 %collective-permute-done.1 = f32[6,128,256]{1,2,0:T(8,128)S(1)} collective-permute-done((f32[6,128,256]{1,2,0:T(8,128)S(1)}, f32[6,128,256]{1,2,0:T(8,128)S(1)}, u32[]{:S(2)}, u32[]{:S(2)}) %collective-permute-start.1) | collective-permute-done | bytes 786464 | tf_op jit(solution)/shard_map/ppermute | solution.py:21
  39.4 0.9 collective-permute-done
  40.3 2.9 %pad_maximum_fusion = f32[44,128,256]{1,2,0:T(8,128)} fusion(f32[6,128,256]{1,2,0:T(8,128)S(1)} %collective-permute-done.1, f32[32,128,256]{1,2,0:T(8,128)S(1)} %select_select_fusion, f32[6,128,256]{1,2,0:T(8,128)S(1)} %collective-permute-done), kind=kLoop, calls=%fused_computation.3 | loop fusion | flops 2883584 | bytes 11534336 | tf_op jit(solution)/shard_map/concatenate | solution.py:22
  43.2 6.3 %copy.17 = f32[44,128,256]{2,1,0:T(8,128)} copy(f32[44,128,256]{1,2,0:T(8,128)} %pad_maximum_fusion) | data formatting | bytes 11534336 | tf_op jit(solution)/shard_map/concatenate | solution.py:22
  49.4 3.3 %slice_bitcast_fusion = f32[128,256,44]{1,0,2:T(8,128)S(1)} fusion(f32[44,128,256]{2,1,0:T(8,128)} %copy.17), kind=kLoop, calls=%fused_computation.2 | loop fusion | bytes 11534336 | tf_op jit(solution)/shard_map/dot_general | solution.py:42
  52.7 8.2 %fusion = f32[32,128,256]{2,0,1:T(8,128)} fusion(f32[128,256,44]{1,0,2:T(8,128)S(1)} %slice_bitcast_fusion, s32[44]{0:T(128)S(1)} %iota_add_fusion.3), kind=kOutput, calls=%fused_computation | convolution fusion | flops 553656576 | bytes 9961648 | tf_op jit(solution)/shard_map/dot_general | solution.py:42
  60.9 0.0 all-gather.2.cloned.1.call-update
  61.0 160.3 %all-gather.2.cloned.1.call-done = f32[32,128,1024]{2,0,1:T(8,128)} async-done(((f32[32,128,256]{2,0,1:T(8,128)}), f32[32,128,1024]{2,0,1:T(8,128)}) %all-gather.2.cloned.1.call-update) | async-done | bytes 16777232 | tf_op jit(solution)/shard_map/all_gather | solution.py:92
  221.3 2.5 constant_dynamic-slice_fusion
  223.8 2.2 fusion.2
  226.0 6.4 %fusion.4 = f32[8,128,8,128]{1,3,2,0:T(8,128)S(1)} fusion(f32[8,128,8,12]{3,0,2,1:T(8,128)S(1)} %bitcast.47, s32[12]{0:T(128)S(1)} %iota_add_fusion.1), kind=kOutput, calls=%fused_computation.8 | convolution fusion | flops 151004160 | bytes 4587568 | tf_op jit(solution)/shard_map/abcd,de->abce/dot_general | solution.py:63
  232.5 6.5 %fusion.8 = f32[8,128,8,128]{1,3,2,0:T(8,128)S(1)} fusion(f32[8,128,8,128]{1,3,2,0:T(8,128)S(1)} %fusion.4, f32[8,128,8,128]{3,0,2,1:T(8,128)S(1)} %get-tuple-element.30, s32[128]{0:T(128)S(1)} %iota_add_fusion.2), kind=kOutput, calls=%fused_computation.16 | convolution fusion | flops 1611759616 | bytes 12583424 | tf_op jit(solution)/shard_map/abcd,de->abce/dot_general | solution.py:56
  239.0 4.4 %convolution_bitcast_fusion = f32[8,140,1024]{2,1,0:T(8,128)S(1)} fusion(f32[8,128,1024]{1,2,0:T(8,128)S(1)} %bitcast.48, s32[128]{0:T(128)S(1)} %iota_add_fusion), kind=kOutput, calls=%fused_computation.15 | convolution fusion | flops 1761715200 | bytes 8782336 | tf_op jit(solution)/shard_map/wy,zyx->zwx/dot_general | solution.py:96
  243.4 0.1 fusion.85
  243.4 1.3 collective-permute-start.2
  244.7 0.1 broadcast_multiply_fusion
  244.8 2.5 slice.86
  247.3 3.1 %collective-permute-start.3 = (f32[8,6,1024]{2,1,0:T(8,128)S(1)}, f32[8,6,1024]{2,1,0:T(8,128)S(1)}, u32[]{:S(2)}, u32[]{:S(2)}) collective-permute-start(f32[8,6,1024]{2,1,0:T(8,128)S(1)} %get-tuple-element.28), channel_id=1, source_target_pairs={{1,0},{3,2},{5,4},{7,6},{9,8},{11,10},{13,12},{15,14},{17,16},{19,... | collective-permute-start | bytes 589832 | tf_op jit(solution)/shard_map/ppermute | solution.py:29
  250.4 0.0 collective-permute-done.2
  250.5 1.8 scatter-add.6
  252.3 0.0 collective-permute-done.3
  252.3 1.0 slice_add_fusion
  253.3 1.7 scatter-add.9
  255.0 6.8 %add_multiply_fusion = (f32[8,128,1024]{2,1,0:T(8,128)}, f32[8,128,1024]{2,1,0:T(8,128)}) fusion(f32[8,128,1024]{2,1,0:T(8,128)} %scatter-add.9, f32[1024]{0:T(1024)S(1)} %fusion.56, f32[8,128]{1,0:T(8,128)S(1)} %broadcast_multiply_fusion), kind=kLoop, calls=%fused_computation.12 | loop fusion | flops 6291456 | bytes 12591104 | tf_op jit(solution)/shard_map/div | solution.py:113
  (11 shorter events, 0.2 us)
Async XLA Ops:
  7.2 5.6 %copy-start = (s32[4,16,32]{2,1,0:T(8,128)S(1)}, s32[4,16,32]{2,1,0:T(8,128)}, u32[]{:S(2)}) copy-start(s32[4,16,32]{2,1,0:T(8,128)} %param.7) | copy-start | bytes 24580
  7.2 214.1 %all-gather.2.cloned.1.call-start = ((), (), s32[]{:S(2)}) async-start(), calls=%async_computation | async-start | bytes 20971520 | tf_op jit(solution)/shard_map/all_gather | solution.py:92
  18.2 21.3 %collective-permute-start.1 = (f32[6,128,256]{1,2,0:T(8,128)S(1)}, f32[6,128,256]{1,2,0:T(8,128)S(1)}, u32[]{:S(2)}, u32[]{:S(2)}) collective-permute-start(f32[6,128,256]{1,2,0:T(8,128)S(1)} %get-tuple-element.33), channel_id=1, source_target_pairs={{8,0},{16,8},{24,16},{9,1},{17,9},{25,17},{10,2},{18,10},{26,18},{... | collective-permute-start | bytes 2359304 | tf_op jit(solution)/shard_map/ppermute | solution.py:21
  19.5 20.9 %collective-permute-start = (f32[6,128,256]{1,2,0:T(8,128)S(1)}, f32[6,128,256]{1,2,0:T(8,128)S(1)}, u32[]{:S(2)}, u32[]{:S(2)}) collective-permute-start(f32[6,128,256]{1,2,0:T(8,128)S(1)} %get-tuple-element.32), channel_id=1, source_target_pairs={{0,8},{8,16},{16,24},{1,9},{9,17},{17,25},{2,10},{10,18},{18,26},{... | collective-permute-start | bytes 2359304 | tf_op jit(solution)/shard_map/ppermute | solution.py:20
  243.4 7.0 %collective-permute-start.2 = (f32[8,6,1024]{2,1,0:T(8,128)S(1)}, f32[8,6,1024]{2,1,0:T(8,128)S(1)}, u32[]{:S(2)}, u32[]{:S(2)}) collective-permute-start(f32[8,6,1024]{2,1,0:T(8,128)S(1)} %get-tuple-element.29), channel_id=1, source_target_pairs={{0,1},{2,3},{4,5},{6,7},{8,9},{10,11},{12,13},{14,15},{16,17},{18,... | collective-permute-start | bytes 589832 | tf_op jit(solution)/shard_map/ppermute | solution.py:29
  247.3 4.9 %collective-permute-start.3 = (f32[8,6,1024]{2,1,0:T(8,128)S(1)}, f32[8,6,1024]{2,1,0:T(8,128)S(1)}, u32[]{:S(2)}, u32[]{:S(2)}) collective-permute-start(f32[8,6,1024]{2,1,0:T(8,128)S(1)} %get-tuple-element.28), channel_id=1, source_target_pairs={{1,0},{3,2},{5,4},{7,6},{9,8},{11,10},{13,12},{15,14},{17,16},{19,... | collective-permute-start | bytes 589832 | tf_op jit(solution)/shard_map/ppermute | solution.py:29
Sparse Core Ops, SparseCore 0:
  61.1 160.2 all-gather.1
where the time goes:
time: 269 us
  waiting for transfers between devices  176 us (65%)
  local copies, waits for them, and re-layouts  28 us (10%)
  matrix products  25.5 us (9%)
  between operations  14.2 us (5%)
  other arithmetic  14.1 us (5%)
  starting transfers between devices  10.4 us (4%)
    all_gather x1, waiting for transfers between devices, body(): gathered = lax.all_gather(physical, 'gx', axis=2, tiled=True)  160 us
    ppermute x1, waiting for transfers between devices, with_halo(): after = lax.ppermute(leading, axis, down)  15.2 us
    dot_general x1, matrix products, along_first(): jnp.dot(kernel, flat, precision=highest, preferred_element_type=jnp.float32)  8.16 us
    div x1, other arithmetic, body(): (top + jnp.tanh(sharpness * (filtered - threshold))) / (top + jnp.tanh(sh...  6.76 us
    dot_general x1, matrix products, filter_last(): jnp.einsum('abcd,de->abce', lower_part, lower_kernel, precision=highest,...  6.49 us
    dot_general x1, matrix products, filter_last(): jnp.einsum('abcd,de->abce', upper_part, upper_kernel, precision=highest,...  6.43 us
    concatenate x1, local copies, waits for them, and re-layouts, with_halo(): x = jnp.concatenate([before, x, after], axis=dim)  6.27 us
    unnamed x3, local copies, waits for them, and re-layouts  5.58 us
  transfers between devices with their start and end apart: 5, of which 3 were waited for; matrix products, arithmetic and copies ran while one was open for 2% of the time, Pallas kernels for 0%

commit v1 on v0

--- a/solution.py
+++ b/solution.py
@@ -89,7 +89,8 @@
     physical = along_first(extended, planes)
     groups = lax.axis_size("gx")
     layers = planes // groups
-    gathered = lax.all_gather(physical, "gx", axis=2, tiled=True)
+    tiles = lax.all_gather(physical, "gx")
+    gathered = jnp.concatenate(tiles, axis=2)
     own_slab = lax.dynamic_slice_in_dim(gathered, lax.axis_index("gx") * layers, layers, 0)
     smoothed = filter_last(own_slab)
     row_kernel = band(row_count + 2 * RADIUS, row_count, RADIUS)

time: 269 us -> 282 us (1.048)
  local copies, waits for them, and re-layouts: 28 us -> 45.9 us
  matrix products: 25.5 us -> 20.2 us
    all_gather x0 -> x1, local copies, waits for them, and re-layouts: none -> 19.4 us  [body(): tiles = lax.all_gather(physical, 'gx')]
    dot_general x1, matrix products: 6.43 us -> 3.53 us  [filter_last(): jnp.einsum('abcd,de->abce', upper_part, upper_kernel, precision=highest,...]
where the time goes in v1:
time: 282 us; the launch traced here: 281 us
  waiting for transfers between devices  177 us (63%)
  local copies, waits for them, and re-layouts  45.9 us (16%)
  matrix products  20.2 us (7%)
  between operations  14.3 us (5%)
  other arithmetic  14.1 us (5%)
  starting transfers between devices  10.4 us (4%)
    all_gather x1, waiting for transfers between devices, body(): tiles = lax.all_gather(physical, 'gx')  160 us
    all_gather x1, local copies, waits for them, and re-layouts, body(): tiles = lax.all_gather(physical, 'gx')  19.4 us
    ppermute x1, waiting for transfers between devices, with_halo(): after = lax.ppermute(leading, axis, down)  15.2 us
    dot_general x1, matrix products, along_first(): jnp.dot(kernel, flat, precision=highest, preferred_element_type=jnp.float32)  8.16 us
    div x1, other arithmetic, body(): (top + jnp.tanh(sharpness * (filtered - threshold))) / (top + jnp.tanh(sh...  6.76 us
    concatenate x1, local copies, waits for them, and re-layouts, with_halo(): x = jnp.concatenate([before, x, after], axis=dim)  6.27 us
  transfers between devices with their start and end apart: 5, of which 3 were waited for; matrix products, arithmetic and copies ran while one was open for 2% of the time, Pallas kernels for 0%

profile of v1, /device:TPU:1, one launch (start us, length us, event | category | flops | bytes accessed | tf_op | source)
XLA Modules:
  0.0 281.4 jit_solution(2288144835151656896)
XLA Ops:
  7.2 0.0 copy-start
  7.2 0.0 all-gather.3.cloned.1.call-start
  7.2 5.6 %copy.14 = f32[32,128,256]{1,2,0:T(8,128)} copy(f32[32,128,256]{2,1,0:T(8,128)} %param.6) | data formatting | bytes 8388608 | tf_op args[0]
  12.8 0.0 copy-done
  12.8 0.3 broadcast_bitcast_fusion
  13.1 0.6 copy.13
  13.8 0.3 broadcast_bitcast_fusion.1
  14.1 0.6 copy.12
  14.8 3.3 %select_select_fusion = f32[32,128,256]{1,2,0:T(8,128)S(1)} fusion(f32[32,128,256]{1,2,0:T(8,128)} %copy.14, pred[32,128,32]{1,2,0:T(8,128)(4,1)S(1)} %copy.13, pred[32,128,32]{1,2,0:T(8,128)(4,1)S(1)} %copy.12), kind=kLoop, calls=%fused_computation.8 | loop fusion | flops 2097152 | bytes 8650752 | tf_op jit(solution)/shard_map/jit(_where)/select_n | solution.py:87
  18.0 0.1 fusion.79
  18.2 1.3 collective-permute-start.1
  19.5 4.7 %collective-permute-start = (f32[6,128,256]{1,2,0:T(8,128)S(1)}, f32[6,128,256]{1,2,0:T(8,128)S(1)}, u32[]{:S(2)}, u32[]{:S(2)}) collective-permute-start(f32[6,128,256]{1,2,0:T(8,128)S(1)} %get-tuple-element.32), channel_id=1, source_target_pairs={{0,8},{8,16},{16,24},{1,9},{9,17},{17,25},{2,10},{10,18},{18,26},{... | collective-permute-start | bytes 2359304 | tf_op jit(solution)/shard_map/ppermute | solution.py:20
  24.2 15.2 %collective-permute-done.1 = f32[6,128,256]{1,2,0:T(8,128)S(1)} collective-permute-done((f32[6,128,256]{1,2,0:T(8,128)S(1)}, f32[6,128,256]{1,2,0:T(8,128)S(1)}, u32[]{:S(2)}, u32[]{:S(2)}) %collective-permute-start.1) | collective-permute-done | bytes 786464 | tf_op jit(solution)/shard_map/ppermute | solution.py:21
  39.4 0.9 collective-permute-done
  40.3 2.9 %pad_maximum_fusion = f32[44,128,256]{1,2,0:T(8,128)} fusion(f32[6,128,256]{1,2,0:T(8,128)S(1)} %collective-permute-done.1, f32[32,128,256]{1,2,0:T(8,128)S(1)} %select_select_fusion, f32[6,128,256]{1,2,0:T(8,128)S(1)} %collective-permute-done), kind=kLoop, calls=%fused_computation.3 | loop fusion | flops 2883584 | bytes 11534336 | tf_op jit(solution)/shard_map/concatenate | solution.py:22
  43.2 6.3 %copy.15 = f32[44,128,256]{2,1,0:T(8,128)} copy(f32[44,128,256]{1,2,0:T(8,128)} %pad_maximum_fusion) | data formatting | bytes 11534336 | tf_op jit(solution)/shard_map/concatenate | solution.py:22
  49.4 3.3 %slice_bitcast_fusion = f32[128,256,44]{1,0,2:T(8,128)S(1)} fusion(f32[44,128,256]{2,1,0:T(8,128)} %copy.15), kind=kLoop, calls=%fused_computation.2 | loop fusion | bytes 11534336 | tf_op jit(solution)/shard_map/dot_general | solution.py:42
  52.7 8.2 %fusion = f32[32,128,256]{2,0,1:T(8,128)} fusion(f32[128,256,44]{1,0,2:T(8,128)S(1)} %slice_bitcast_fusion, s32[44]{0:T(128)S(1)} %iota_add_fusion.3), kind=kOutput, calls=%fused_computation | convolution fusion | flops 553656576 | bytes 9961648 | tf_op jit(solution)/shard_map/dot_general | solution.py:42
  60.9 0.0 all-gather.3.cloned.1.call-update
  61.0 160.4 %all-gather.3.cloned.1.call-done = f32[128,128,256]{2,0,1:T(8,128)} async-done(((f32[32,128,256]{2,0,1:T(8,128)}), f32[128,128,256]{2,0,1:T(8,128)}) %all-gather.3.cloned.1.call-update) | async-done | bytes 16777232 | tf_op jit(solution)/shard_map/all_gather | solution.py:92
  221.4 19.4 %copy.17 = f32[4,32,128,256]{2,3,0,1:T(8,128)} copy(f32[4,32,128,256]{3,1,0,2:T(8,128)} %bitcast.51) | data formatting | bytes 33554432 | tf_op jit(solution)/shard_map/all_gather | solution.py:92
  240.9 2.5 constant_dynamic-slice_fusion
  243.4 0.7 pad_slice_fusion.1
  244.1 3.5 %fusion.2 = f32[8,128,8,128]{1,3,2,0:T(8,128)S(1)} fusion(f32[8,128,8,128]{1,3,2,0:T(8,128)S(1)} %bitcast.53, s32[12]{0:T(128)S(1)} %iota_add_fusion.1), kind=kOutput, calls=%fused_computation.13 | convolution fusion | flops 151004160 | bytes 4719104 | tf_op jit(solution)/shard_map/abcd,de->abce/dot_general | solution.py:63
  247.6 3.9 %convolution_add_fusion = f32[8,128,8,128]{1,3,2,0:T(8,128)S(1)} fusion(f32[8,128,8,128]{1,3,2,0:T(8,128)S(1)} %fusion.2, f32[8,128,8,128]{1,3,2,0:T(8,128)S(1)} %bitcast.50, s32[128]{0:T(128)S(1)} %iota_add_fusion.2), kind=kOutput, calls=%fused_computation.10 | convolution fusion | flops 1611759616 | bytes 12583424 | tf_op jit(solution)/shard_map/abcd,de->abce/dot_general | solution.py:56
  251.5 4.6 %convolution_bitcast_fusion = f32[8,140,1024]{2,1,0:T(8,128)S(1)} fusion(f32[8,128,1024]{1,2,0:T(8,128)S(1)} %bitcast.52, s32[128]{0:T(128)S(1)} %iota_add_fusion), kind=kOutput, calls=%fused_computation.9 | convolution fusion | flops 1761715200 | bytes 8782336 | tf_op jit(solution)/shard_map/wy,zyx->zwx/dot_general | solution.py:97
  256.2 0.1 fusion.78
  256.2 1.3 collective-permute-start.2
  257.5 0.1 broadcast_multiply_fusion
  257.6 2.5 slice.86
  260.1 3.1 %collective-permute-start.3 = (f32[8,6,1024]{2,1,0:T(8,128)S(1)}, f32[8,6,1024]{2,1,0:T(8,128)S(1)}, u32[]{:S(2)}, u32[]{:S(2)}) collective-permute-start(f32[8,6,1024]{2,1,0:T(8,128)S(1)} %get-tuple-element.28), channel_id=1, source_target_pairs={{1,0},{3,2},{5,4},{7,6},{9,8},{11,10},{13,12},{15,14},{17,16},{19,... | collective-permute-start | bytes 589832 | tf_op jit(solution)/shard_map/ppermute | solution.py:29
  263.2 0.0 collective-permute-done.2
  263.3 1.8 scatter-add.6
  265.1 0.0 collective-permute-done.3
  265.1 1.0 slice_add_fusion
  266.1 1.7 scatter-add.9
  267.8 6.8 %add_multiply_fusion = (f32[8,128,1024]{2,1,0:T(8,128)}, f32[8,128,1024]{2,1,0:T(8,128)}) fusion(f32[8,128,1024]{2,1,0:T(8,128)} %scatter-add.9, f32[1024]{0:T(1024)S(1)} %fusion.49, f32[8,128]{1,0:T(8,128)S(1)} %broadcast_multiply_fusion), kind=kLoop, calls=%fused_computation.6 | loop fusion | flops 6291456 | bytes 12591104 | tf_op jit(solution)/shard_map/div | solution.py:114
  (11 shorter events, 0.2 us)
Async XLA Ops:
  7.2 5.6 %copy-start = (s32[4,16,32]{2,1,0:T(8,128)S(1)}, s32[4,16,32]{2,1,0:T(8,128)}, u32[]{:S(2)}) copy-start(s32[4,16,32]{2,1,0:T(8,128)} %param.7) | copy-start | bytes 24580
  7.2 214.3 %all-gather.3.cloned.1.call-start = ((), (), s32[]{:S(2)}) async-start(), calls=%async_computation | async-start | bytes 20971520 | tf_op jit(solution)/shard_map/all_gather | solution.py:92
  18.2 21.3 %collective-permute-start.1 = (f32[6,128,256]{1,2,0:T(8,128)S(1)}, f32[6,128,256]{1,2,0:T(8,128)S(1)}, u32[]{:S(2)}, u32[]{:S(2)}) collective-permute-start(f32[6,128,256]{1,2,0:T(8,128)S(1)} %get-tuple-element.33), channel_id=1, source_target_pairs={{8,0},{16,8},{24,16},{9,1},{17,9},{25,17},{10,2},{18,10},{26,18},{... | collective-permute-start | bytes 2359304 | tf_op jit(solution)/shard_map/ppermute | solution.py:21
  19.5 20.9 %collective-permute-start = (f32[6,128,256]{1,2,0:T(8,128)S(1)}, f32[6,128,256]{1,2,0:T(8,128)S(1)}, u32[]{:S(2)}, u32[]{:S(2)}) collective-permute-start(f32[6,128,256]{1,2,0:T(8,128)S(1)} %get-tuple-element.32), channel_id=1, source_target_pairs={{0,8},{8,16},{16,24},{1,9},{9,17},{17,25},{2,10},{10,18},{18,26},{... | collective-permute-start | bytes 2359304 | tf_op jit(solution)/shard_map/ppermute | solution.py:20
  256.2 7.0 %collective-permute-start.2 = (f32[8,6,1024]{2,1,0:T(8,128)S(1)}, f32[8,6,1024]{2,1,0:T(8,128)S(1)}, u32[]{:S(2)}, u32[]{:S(2)}) collective-permute-start(f32[8,6,1024]{2,1,0:T(8,128)S(1)} %get-tuple-element.29), channel_id=1, source_target_pairs={{0,1},{2,3},{4,5},{6,7},{8,9},{10,11},{12,13},{14,15},{16,17},{18,... | collective-permute-start | bytes 589832 | tf_op jit(solution)/shard_map/ppermute | solution.py:29
  260.1 4.9 %collective-permute-start.3 = (f32[8,6,1024]{2,1,0:T(8,128)S(1)}, f32[8,6,1024]{2,1,0:T(8,128)S(1)}, u32[]{:S(2)}, u32[]{:S(2)}) collective-permute-start(f32[8,6,1024]{2,1,0:T(8,128)S(1)} %get-tuple-element.28), channel_id=1, source_target_pairs={{1,0},{3,2},{5,4},{7,6},{9,8},{11,10},{13,12},{15,14},{17,16},{19,... | collective-permute-start | bytes 589832 | tf_op jit(solution)/shard_map/ppermute | solution.py:29
Sparse Core Ops, SparseCore 0:
  61.1 160.3 all-gather.2
